TPU v7x, 32 devices: a whole 2x2x4 slice. The times are simulated.
32 devices in a mesh: expert: 4 (over y, x), shard: 8 (over z, core).
Axes of the slice: x: 2, y: 2, z: 4, core: 2. Of those that a mesh axis runs over, the one named last changes fastest.
Arguments:
- master_gate: float32 [128, 2048, 768], P('expert', 'shard'), may hold values from -0.1875 to 0.1875
- master_up: float32 [128, 2048, 768], P('expert', 'shard'), may hold values from -0.1875 to 0.1875
- router_weight: float32 [2048, 128], P('shard', 'expert'), may hold values from -0.125 to 0.125
- router_gain: float32 [2048], P('shard'), may hold values from 0.25 to 1.75
Outputs:
- final_gate: bfloat16 [128, 2048, 768], P(('expert', 'shard'))
- final_up: bfloat16 [128, 2048, 768], P(('expert', 'shard'))
- scale_gate: float32 [128, 768], P(('expert', 'shard'))
- scale_up: float32 [128, 768], P(('expert', 'shard'))
- serve_router: bfloat16 [2048, 128], replicated
All inputs are finite; a program needn't handle non-finite values. Where the computation divides by a largest or mean magnitude, that divisor is 1e-20 or more.
Results may differ from a plain program's by a relative error of at most 0.001.
Values may be sent and summed in bfloat16 or wider, within the bound.
A program may use at most 192 MiB of HBM per device.

v0:
```python
import jax
import jax.numpy as jnp
from jax import lax
from jax.sharding import PartitionSpec as P

D_MODEL = 2048


def body(master_gate, master_up, router_weight, router_gain):
    total_gate, total_up = lax.psum(
        (jnp.sum(jnp.abs(master_gate), axis=1), jnp.sum(jnp.abs(master_up), axis=1)), "shard"
    )
    scale_gate = total_gate / D_MODEL
    scale_up = total_up / D_MODEL
    narrow_gate, narrow_up = (
        (master_gate / jnp.expand_dims(scale_gate, 1)).astype(jnp.bfloat16),
        (master_up / jnp.expand_dims(scale_up, 1)).astype(jnp.bfloat16),
    )
    final_gate, final_up = (
        lax.all_to_all(narrow_gate, "shard", split_axis=0, concat_axis=1, tiled=True),
        lax.all_to_all(narrow_up, "shard", split_axis=0, concat_axis=1, tiled=True),
    )
    scale_gate = lax.dynamic_slice_in_dim(
        scale_gate, lax.axis_index("shard") * final_gate.shape[0], final_gate.shape[0], axis=0
    )
    scale_up = lax.dynamic_slice_in_dim(
        scale_up, lax.axis_index("shard") * final_up.shape[0], final_up.shape[0], axis=0
    )
    part_router = (router_weight * router_gain[:, None]).astype(jnp.bfloat16)
    row_router = lax.all_gather(part_router, "shard", axis=0, tiled=True)
    serve_router = lax.all_gather(row_router, "expert", axis=1, tiled=True)
    return (final_gate, final_up, scale_gate, scale_up, serve_router)


def solution(mesh):
    return jax.shard_map(
        body,
        mesh=mesh,
        in_specs=(
            P("expert", "shard", None),
            P("expert", "shard", None),
            P("shard", "expert"),
            P("shard"),
        ),
        out_specs=(
            P(("expert", "shard"), None, None),
            P(("expert", "shard"), None, None),
            P(("expert", "shard"), None),
            P(("expert", "shard"), None),
            P(),
        ),
        check_vma=False,
    )
```

profile of v0, /device:TPU:1, one launch (start us, length us, event | category | flops | bytes accessed | tf_op | source)
XLA Modules:
  0.0 701.1 jit_solution(948613647621270715)
XLA Ops:
  7.2 0.0 all-reduce.3.cloned.1.call-start
  7.2 17.4 %abs_reduce_fusion = (f32[32,768]{1,0:T(8,128)}, f32[32,768]{1,0:T(8,128)}) fusion(f32[32,256,768]{2,1,0:T(8,128)} %param.5, f32[32,256,768]{2,1,0:T(8,128)} %param.4), kind=kLoop, calls=%fused_computation.1 | loop fusion | flops 25116672 | bytes 50528256 | tf_op jit(solution)/shard_map/reduce_sum | solution.py:11
  24.6 0.0 all-reduce.3.cloned.1.call-update
  24.7 55.9 %all-reduce.3.cloned.1.call-done = (f32[32,768]{1,0:T(8,128)}, f32[32,768]{1,0:T(8,128)}) async-done(((f32[32,768]{1,0:T(8,128)}, f32[32,768]{1,0:T(8,128)}), (f32[32,768]{1,0:T(8,128)}, f32[32,768]{1,0:T(8,128)})) %all-reduce.3.cloned.1.call-update) | async-done | bytes 196624 | tf_op jit(solution)/shard_map/psum | solution.py:10
  80.5 0.9 broadcast_multiply_fusion.1
  81.4 0.0 copy-start
  81.4 13.7 %divide_convert_fusion.1 = bf16[32,256,768]{2,1,0:T(8,128)(2,1)} fusion(f32[32,256,768]{2,1,0:T(8,128)} %param.4, f32[32,768]{1,0:T(8,128)S(1)} %broadcast_multiply_fusion.1), kind=kLoop, calls=%fused_computation.2 | loop fusion | flops 12582912 | bytes 37847040 | tf_op jit(solution)/shard_map/convert_element_type | solution.py:16
  95.1 7.6 %all-to-all-start = ((bf16[32,256,768]{2,1,0:T(8,128)(2,1)}), bf16[32,256,768]{2,1,0:T(8,128)(2,1)}, u32[]{:S(2)}, u32[]{:S(2)}) async-start(bf16[32,256,768]{2,1,0:T(8,128)(2,1)} %divide_convert_fusion.1), calls=%async_computation | async-start | bytes 25165824 | tf_op jit(solution)/shard_map/all_to_all | solution.py:20
  102.7 0.0 copy-done
  102.8 0.0 copy-start.1
  102.8 0.0 copy-start.2
  102.8 13.8 %divide_convert_fusion = bf16[32,256,768]{2,1,0:T(8,128)(2,1)} fusion(f32[32,256,768]{2,1,0:T(8,128)} %param.5, f32[32,768]{1,0:T(8,128)S(1)} %broadcast_multiply_fusion), kind=kLoop, calls=%fused_computation | loop fusion | flops 12582912 | bytes 37847040 | tf_op jit(solution)/shard_map/convert_element_type | solution.py:17
  116.6 259.1 %all-to-all-done = bf16[32,256,768]{2,1,0:T(8,128)(2,1)} async-done(((bf16[32,256,768]{2,1,0:T(8,128)(2,1)}), bf16[32,256,768]{2,1,0:T(8,128)(2,1)}, u32[]{:S(2)}, u32[]{:S(2)}) %all-to-all-start) | async-done | bytes 12582944 | tf_op jit(solution)/shard_map/all_to_all | solution.py:20
  375.6 6.2 all-to-all-start.1
  381.9 0.0 copy-done.1
  381.9 0.0 copy-done.2
  381.9 279.9 %all_gather.6 = bf16[2048,32]{0,1:T(8,128)(2,1)S(1)} all-gather(bf16[256,32]{0,1:T(8,128)(2,1)S(1)} %multiply_convert_fusion), channel_id=1, replica_groups=mesh['expert'=4,'shard'=8] {'shard'}, dimensions={0}, use_global_device_ids=true | all-gather | bytes 147456 | tf_op jit(solution)/shard_map/all_gather | solution.py:30
  661.8 8.8 %all_gather.7 = bf16[2048,128]{0,1:T(8,128)(2,1)S(1)} all-gather(bf16[2048,32]{0,1:T(8,128)(2,1)S(1)} %all_gather.6), channel_id=1, replica_groups=mesh['expert'=4,'shard'=8] {'expert'}, dimensions={1}, use_global_device_ids=true | all-gather | bytes 655360 | tf_op jit(solution)/shard_map/all_gather | solution.py:31
  670.7 1.0 copy.14
  671.7 0.6 constant_dynamic-slice_fusion
  672.3 0.6 constant_dynamic-slice_fusion.1
  672.9 10.7 %copy.12 = bf16[8,4,256,768]{3,2,0,1:T(8,128)(2,1)} copy(bf16[8,4,256,768]{3,2,1,0:T(8,128)(2,1)} %bitcast) | data formatting | bytes 25165824 | tf_op jit(solution)/shard_map/all_to_all | solution.py:20
  683.6 0.0 all-to-all-done.1
  683.6 10.7 %copy.13 = bf16[8,4,256,768]{3,2,0,1:T(8,128)(2,1)} copy(bf16[8,4,256,768]{3,2,1,0:T(8,128)(2,1)} %bitcast.3) | data formatting | bytes 25165824 | tf_op jit(solution)/shard_map/all_to_all | solution.py:21
  (2 shorter events, 0.0 us)
Async XLA Ops:
  7.2 73.4 %all-reduce.3.cloned.1.call-start = ((), (), s32[]{:S(2)}) async-start(), calls=%async_computation.2 | async-start | bytes 393216 | tf_op jit(solution)/shard_map/psum | solution.py:10
  81.4 21.3 %copy-start = (f32[32,768]{1,0:T(8,128)S(1)}, f32[32,768]{1,0:T(8,128)}, u32[]{:S(2)}) copy-start(f32[32,768]{1,0:T(8,128)} %get-tuple-element.11) | copy-start | bytes 294916
  95.1 280.5 %all-to-all-start = ((bf16[32,256,768]{2,1,0:T(8,128)(2,1)}), bf16[32,256,768]{2,1,0:T(8,128)(2,1)}, u32[]{:S(2)}, u32[]{:S(2)}) async-start(bf16[32,256,768]{2,1,0:T(8,128)(2,1)} %divide_convert_fusion.1), calls=%async_computation | async-start | bytes 25165824 | tf_op jit(solution)/shard_map/all_to_all | solution.py:20
  102.8 279.1 %copy-start.1 = (f32[256,32]{0,1:T(8,128)S(1)}, f32[256,32]{0,1:T(8,128)}, u32[]{:S(2)}) copy-start(f32[256,32]{0,1:T(8,128)} %param.6) | copy-start | bytes 98308
  102.8 279.1 %copy-start.2 = (f32[256]{0:T(256)S(1)}, f32[256]{0:T(256)}, u32[]{:S(2)}) copy-start(f32[256]{0:T(256)} %param.7) | copy-start | bytes 3076
  375.6 307.9 %all-to-all-start.1 = ((bf16[32,256,768]{2,1,0:T(8,128)(2,1)}), bf16[32,256,768]{2,1,0:T(8,128)(2,1)}, u32[]{:S(2)}, u32[]{:S(2)}) async-start(bf16[32,256,768]{2,1,0:T(8,128)(2,1)} %divide_convert_fusion), calls=%async_computation.1 | async-start | bytes 25165824 | tf_op jit(solution)/shard_map/all_to_all | solution.py:21
Sparse Core Ops, SparseCore 0:
  24.8 55.6 all-reduce.2
where the time goes:
time: 703 us; the launch traced here: 701 us
  waiting for transfers between devices  315 us (45%)
  blocking collectives  289 us (41%)
  other arithmetic  45.8 us (7%)
  local copies, waits for them, and re-layouts  23.6 us (3%)
  between operations  14.1 us (2%)
  starting transfers between devices  13.9 us (2%)
    all_gather x1, blocking collectives, body(): row_router = lax.all_gather(part_router, 'shard', axis=0, tiled=True)  280 us
    all_to_all x1, waiting for transfers between devices, body(): lax.all_to_all(narrow_gate, 'shard', split_axis=0, concat_axis=1, tiled=T...  259 us
    psum x1, waiting for transfers between devices, body(): lax.psum((jnp.sum(jnp.abs(master_gate), axis=1), jnp.sum(jnp.abs(master_u...  55.9 us
    reduce_sum x1, other arithmetic, body(): jnp.sum(jnp.abs(master_up), axis=1)  17.4 us
  transfers between devices with their start and end apart: 3, of which 2 were waited for; matrix products, arithmetic and copies ran while one was open for 4% of the time, Pallas kernels for 0%

commit v1 on v0

v1 whole, which is shorter than its diff:
```python
import functools

import jax
import jax.numpy as jnp
from jax import lax
from jax.experimental import pallas as pl
from jax.experimental.pallas import tpu as pltpu
from jax.sharding import PartitionSpec as P

MESH = pl.DeviceIdType.MESH
SLOTS = 4
LEAD = 4


def sum_order(n):
    chips = n // 2
    return sorted(range(n), key=lambda g: (abs(2 * (g // 2) - (chips - 1)), g % 2, g))


def send_order(n, me):
    chip = me // 2
    order = sum_order(n)
    others = [g for g in range(n) if g // 2 != chip]
    return sorted(others, key=lambda g: (abs(g // 2 - chip), g % 2, order.index(g)))


def pick(me, values):
    result = jnp.int32(values[0])
    for i in range(1, len(values)):
        result = jnp.where(me == i, jnp.int32(values[i]), result)
    return result


def kernel(
    n, ne, rows_total,
    gate, up, router_t, gain,
    final_gate, final_up, scale_gate, scale_up, out_router_t,
    ring, sbuf, psum, parts, scales, routers,
    read_sem, psum_send, psum_recv, scale_send, scale_recv,
    data_send, data_recv, row_send, row_recv, col_send, col_recv,
):
    me = lax.axis_index("shard")
    mine = lax.axis_index("expert")
    per = final_gate.shape[0]
    rows, cols = gate.shape[1], gate.shape[2]
    sources, finals = (gate, up), (final_gate, final_up)

    order = sum_order(n)
    tables = [send_order(n, i) for i in range(n)]
    remote = [pick(me, [tables[i][k] for i in range(n)]) for k in range(n - 2)]
    partner = me + 1 - 2 * lax.rem(me, 2)
    targets = [remote[0], partner, me] + remote[1:]

    work = []
    for i in range(LEAD):
        work += [("sum", i, order[i], t) for t in (0, 1)]
    work += [("send", 0, targets[0], t) for t in (0, 1)]
    for i in range(LEAD, n):
        work += [("sum", i, order[i], t) for t in (0, 1)]
    for k in range(1, n):
        work += [("send", k, targets[k], t) for t in (0, 1)]

    def read(index):
        _, _, group, t = work[index]
        slot = index % SLOTS
        return pltpu.make_async_copy(
            sources[t].at[pl.ds(group * per, per)], ring.at[slot], read_sem.at[slot]
        )

    for index in range(SLOTS):
        read(index).start()

    def peer(j):
        return lax.rem(me + j, n)

    def other(j):
        return lax.rem(mine + j, ne)

    def psum_copy(group):
        return pltpu.make_async_remote_copy(
            src_ref=psum.at[group], dst_ref=parts.at[me], send_sem=psum_send.at[group],
            recv_sem=psum_recv.at[me], device_id={"shard": group}, device_id_type=MESH,
        )

    def psum_arrival(source):
        return pltpu.make_async_remote_copy(
            src_ref=parts.at[source], dst_ref=parts.at[source], send_sem=psum_send.at[source],
            recv_sem=psum_recv.at[source], device_id={"shard": source}, device_id_type=MESH,
        )

    def scale_copy(j):
        return pltpu.make_async_remote_copy(
            src_ref=scales.at[me], dst_ref=scales.at[me], send_sem=scale_send.at[j],
            recv_sem=scale_recv.at[me], device_id={"shard": peer(j)}, device_id_type=MESH,
        )

    def scale_arrival(group):
        return pltpu.make_async_remote_copy(
            src_ref=scales.at[group], dst_ref=scales.at[group], send_sem=scale_send.at[0],
            recv_sem=scale_recv.at[group], device_id={"shard": group}, device_id_type=MESH,
        )

    def data_copy(k, t, e):
        return pltpu.make_async_remote_copy(
            src_ref=sbuf.at[k, t * per + e],
            dst_ref=finals[t].at[e, pl.ds(me * rows, rows)],
            send_sem=data_send.at[k, t * per + e],
            recv_sem=data_recv.at[me, t * per + e],
            device_id={"shard": targets[k]}, device_id_type=MESH,
        )

    def own_copy(k, t, e):
        return pltpu.make_async_copy(
            sbuf.at[k, t * per + e],
            finals[t].at[e, pl.ds(me * rows, rows)],
            data_send.at[k, t * per + e],
        )

    def data_arrival(source, t, e):
        return pltpu.make_async_remote_copy(
            src_ref=finals[t].at[e, pl.ds(source * rows, rows)],
            dst_ref=finals[t].at[e, pl.ds(source * rows, rows)],
            send_sem=data_send.at[0, t * per + e],
            recv_sem=data_recv.at[source, t * per + e],
            device_id={"shard": source}, device_id_type=MESH,
        )

    def row_copy(j):
        return pltpu.make_async_remote_copy(
            src_ref=routers.at[mine, me], dst_ref=routers.at[mine, me], send_sem=row_send.at[j],
            recv_sem=row_recv.at[me], device_id={"shard": peer(j)}, device_id_type=MESH,
        )

    def row_arrival(source):
        return pltpu.make_async_remote_copy(
            src_ref=routers.at[mine, source], dst_ref=routers.at[mine, source],
            send_sem=row_send.at[0], recv_sem=row_recv.at[source],
            device_id={"shard": source}, device_id_type=MESH,
        )

    def col_copy(j):
        return pltpu.make_async_remote_copy(
            src_ref=routers.at[mine], dst_ref=routers.at[mine], send_sem=col_send.at[j],
            recv_sem=col_recv.at[mine], device_id={"expert": other(j)}, device_id_type=MESH,
        )

    def col_arrival(source):
        return pltpu.make_async_remote_copy(
            src_ref=routers.at[source], dst_ref=routers.at[source], send_sem=col_send.at[0],
            recv_sem=col_recv.at[source], device_id={"expert": source}, device_id_type=MESH,
        )

    barrier = pltpu.get_barrier_semaphore()
    for j in range(1, n):
        pl.semaphore_signal(barrier, inc=1, device_id={"shard": peer(j)}, device_id_type=MESH)
    for j in range(1, ne):
        pl.semaphore_signal(barrier, inc=1, device_id={"expert": other(j)}, device_id_type=MESH)

    def sum_chunk(slot, group, t):
        def one(e, _):
            def block(b, total):
                start = pl.multiple_of(b * 8, 8)
                return total + jnp.abs(ring[slot, e, pl.ds(start, 8), :])

            total = lax.fori_loop(
                0, rows // 8, block, jnp.zeros((8, cols), jnp.float32), unroll=8
            )
            psum[group, pl.ds(t * per + e, 1), :] = jnp.sum(total, axis=0, keepdims=True)
            return 0

        lax.fori_loop(0, per, one, 0)

    def send_chunk(slot, k, group, t):
        def one(e, _):
            inverse = 1.0 / scales[group, pl.ds(t * per + e, 1), :]
            wide = jnp.broadcast_to(inverse, (16, cols))

            def block(b, _):
                start = pl.multiple_of(b * 16, 16)
                sbuf[k, t * per + e, pl.ds(start, 16), :] = (
                    ring[slot, e, pl.ds(start, 16), :] * wide
                ).astype(jnp.bfloat16)
                return 0

            lax.fori_loop(0, rows // 16, block, 0, unroll=4)
            if k == 2:
                own_copy(k, t, e).start()
            else:
                data_copy(k, t, e).start()
            return 0

        lax.fori_loop(0, per, one, 0)

    def home():
        for j in range(1, n):
            psum_arrival(peer(j)).wait_recv()
        parts[me] = psum[me]
        total = parts[0]
        for i in range(1, n):
            total = total + parts[i]
        scale = total / rows_total
        scales[me] = scale
        for j in range(1, n):
            scale_copy(j).start()
        scale_gate[...] = scale[:per]
        scale_up[...] = scale[per:]

    early = me == order[0]
    for i in range(1, LEAD // 2):
        early = jnp.logical_or(early, me == order[i])

    for index, (kind, step, group, t) in enumerate(work):
        slot = index % SLOTS
        if kind == "send" and t == 0:
            if step == 0:
                pl.when(early)(home)
            elif step == 1:
                pl.when(jnp.logical_not(early))(home)
                routers[mine, me] = (router_t[...] * gain[...]).astype(jnp.bfloat16)
                for j in range(1, n):
                    row_copy(j).start()
            if step != 2:
                scale_arrival(group).wait_recv()
        read(index).wait()
        if kind == "sum":
            sum_chunk(slot, group, t)
            if t == 1:
                if step == 0:
                    pl.semaphore_wait(barrier, n - 1 + ne - 1)

                @pl.when(me != group)
                def _(group=group):
                    psum_copy(group).start()
        else:
            send_chunk(slot, step, group, t)
        if index + SLOTS < len(work):
            read(index + SLOTS).start()

    for j in range(1, n):
        row_arrival(peer(j)).wait_recv()
    for j in range(1, ne):
        col_copy(j).start()
    for j in range(1, ne):
        col_arrival(other(j)).wait_recv()
    wide, tall = routers.shape[2], routers.shape[3]
    for e in range(ne):
        for s in range(n):
            out_router_t[e * wide:(e + 1) * wide, s * tall:(s + 1) * tall] = routers[e, s]

    for j in range(1, n):
        psum_copy(peer(j)).wait_send()
        scale_copy(j).wait_send()
        row_copy(j).wait_send()
    for j in range(1, ne):
        col_copy(j).wait_send()
    for k in range(n):
        for t in (0, 1):

            def done(e, _, k=k, t=t):
                if k == 2:
                    own_copy(k, t, e).wait()
                else:
                    data_copy(k, t, e).wait_send()
                return 0

            lax.fori_loop(0, per, done, 0)
    for j in range(1, n):
        for t in (0, 1):

            def arrived(e, _, j=j, t=t):
                data_arrival(peer(j), t, e).wait_recv()
                return 0

            lax.fori_loop(0, per, arrived, 0)


def solution(mesh):
    n, ne = mesh.shape["shard"], mesh.shape["expert"]

    def body(master_gate, master_up, router_weight, router_gain):
        held, rows, cols = master_gate.shape
        per = held // n
        router_t = router_weight.T
        wide, tall = router_t.shape
        sem = pltpu.SemaphoreType.DMA
        final_gate, final_up, scale_gate, scale_up, serve_t = pl.pallas_call(
            functools.partial(kernel, n, ne, rows * n),
            out_shape=(
                jax.ShapeDtypeStruct((per, rows * n, cols), jnp.bfloat16),
                jax.ShapeDtypeStruct((per, rows * n, cols), jnp.bfloat16),
                jax.ShapeDtypeStruct((per, cols), jnp.float32),
                jax.ShapeDtypeStruct((per, cols), jnp.float32),
                jax.ShapeDtypeStruct((wide * ne, tall * n), jnp.bfloat16),
            ),
            in_specs=[
                pl.BlockSpec(memory_space=pl.ANY),
                pl.BlockSpec(memory_space=pl.ANY),
                pl.BlockSpec(memory_space=pltpu.VMEM),
                pl.BlockSpec(memory_space=pltpu.VMEM),
            ],
            out_specs=(
                pl.BlockSpec(memory_space=pl.ANY),
                pl.BlockSpec(memory_space=pl.ANY),
                pl.BlockSpec(memory_space=pltpu.VMEM),
                pl.BlockSpec(memory_space=pltpu.VMEM),
                pl.BlockSpec(memory_space=pltpu.VMEM),
            ),
            scratch_shapes=[
                pltpu.VMEM((SLOTS, per, rows, cols), jnp.float32),
                pltpu.VMEM((n, 2 * per, rows, cols), jnp.bfloat16),
                pltpu.VMEM((n, 2 * per, cols), jnp.float32),
                pltpu.VMEM((n, 2 * per, cols), jnp.float32),
                pltpu.VMEM((n, 2 * per, cols), jnp.float32),
                pltpu.VMEM((ne, n, wide, tall), jnp.bfloat16),
                sem((SLOTS,)),
                sem((n,)), sem((n,)), sem((n,)), sem((n,)),
                sem((n, 2 * per)), sem((n, 2 * per)),
                sem((n,)), sem((n,)), sem((ne,)), sem((ne,)),
            ],
            compiler_params=pltpu.CompilerParams(
                collective_id=0, has_side_effects=True, vmem_limit_bytes=60 * 1024 * 1024
            ),
        )(master_gate, master_up, router_t, router_gain[None, :])
        return final_gate, final_up, scale_gate, scale_up, serve_t.T

    return jax.shard_map(
        body,
        mesh=mesh,
        in_specs=(
            P("expert", "shard", None),
            P("expert", "shard", None),
            P("shard", "expert"),
            P("shard"),
        ),
        out_specs=(
            P(("expert", "shard"), None, None),
            P(("expert", "shard"), None, None),
            P(("expert", "shard"), None),
            P(("expert", "shard"), None),
            P(),
        ),
        check_vma=False,
    )
```

time: 703 us -> 593 us (0.84)
  Pallas kernels: 0 us -> 571 us
  waiting for transfers between devices: 315 us -> 0 us
  blocking collectives: 289 us -> 0 us
  other arithmetic: 45.8 us -> 0 us
  starting transfers between devices: 13.9 us -> 0 us
  between operations: 14.1 us -> 0.65 us
    pallas_call x0 -> x1, Pallas kernels: none -> 571 us  [body(): pl.pallas_call(functools.partial(kernel, n, ne, rows * n), out_shape=(jax...]
    all_gather x2 -> x0, blocking collectives: 289 us -> none  [the longest x1 280 us: body(): row_router = lax.all_gather(part_router, 'shard', axis=0, tiled=True)]
    all_to_all x2 -> x0, waiting for transfers between devices: 259 us -> none  [the longest x1 259 us: body(): lax.all_to_all(narrow_gate, 'shard', split_axis=0, concat_axis=1, tiled=T...]
    psum x1 -> x0, waiting for transfers between devices: 55.9 us -> none  [body(): lax.psum((jnp.sum(jnp.abs(master_gate), axis=1), jnp.sum(jnp.abs(master_u...]
    convert_element_type x3 -> x0, other arithmetic: 27.5 us -> none  [the longest x1 13.8 us: body(): (master_up / jnp.expand_dims(scale_up, 1)).astype(jnp.bfloat16)]
    all_to_all x2 -> x0, local copies, waits for them, and re-layouts: 21.4 us -> none  [the longest x1 10.7 us: body(): lax.all_to_all(narrow_up, 'shard', split_axis=0, concat_axis=1, tiled=True)]
    unnamed x7 -> x11, local copies, waits for them, and re-layouts: 1.02 us -> 21 us
    reduce_sum x1 -> x0, other arithmetic: 17.4 us -> none  [body(): jnp.sum(jnp.abs(master_up), axis=1)]
  transfers between devices with their start and end apart: 3 -> 0, of which waited for: 2 -> 0; matrix products, arithmetic and copies ran while one was open for 4% -> 0% of each run, Pallas kernels for 0% -> 0%
where the time goes in v1:
time: 593 us; the launch traced here: 592 us
  Pallas kernels  571 us (96%)
  local copies, waits for them, and re-layouts  21 us (4%)
    pallas_call x1, Pallas kernels, body(): pl.pallas_call(functools.partial(kernel, n, ne, rows * n), out_shape=(jax...  571 us
    unnamed x11, local copies, waits for them, and re-layouts  21 us

profile of v1, /device:TPU:1, one launch (start us, length us, event | category | flops | bytes accessed | tf_op | source)
XLA Modules:
  0.0 592.4 jit_solution(8234921172186448981)
XLA Ops:
  0.6 570.8 %shard_map.83 = (bf16[4,2048,768]{2,1,0:T(8,128)(2,1)}, bf16[4,2048,768]{2,1,0:T(8,128)(2,1)}, f32[4,768]{1,0:T(4,128)}, f32[4,768]{1,0:T(4,128)}, bf16[128,2048]{1,0:T(8,128)(2,1)}) custom-call(f32[32,256,768]{2,1,0:T(8,128)} %gate.1, f32[32,256,768]{2,1,0:T(8,128)} %up.1, f32[32,256]{1,0:T(8,128)} %bitcast.4, f32[1,256]{1,0:T(1,128)} %bitcast.5), custom_call_target="tpu_custom_call" | custom-call | tf_op jit(solution)/shard_map/pallas_call | solution.py:286
  571.4 2.0 copy.9
  573.4 0.0 copy-start
  573.4 11.0 %copy.14 = bf16[4,2048,768]{2,1,0:T(8,128)(2,1)} copy(bf16[4,2048,768]{2,1,0:T(8,128)(2,1)} %get-tuple-element.25) | data formatting | bytes 25165824
  584.4 2.0 copy-done
  586.4 0.0 copy-start.2
  586.4 0.0 copy-start.1
  586.4 4.8 copy.15
  591.2 0.0 copy-done.2
  591.2 0.6 copy.16
  591.8 0.0 copy-done.1
  591.8 0.6 copy.17
Async XLA Ops:
  573.4 13.0 %copy-start = (bf16[4,2048,768]{2,1,0:T(8,128)(2,1)S(1)}, bf16[4,2048,768]{2,1,0:T(8,128)(2,1)}, u32[]{:S(2)}) copy-start(bf16[4,2048,768]{2,1,0:T(8,128)(2,1)} %get-tuple-element.26) | copy-start | bytes 37748740
  586.4 4.8 copy-start.2
  586.4 5.4 copy-start.1

commit v2 on v1

--- a/solution.py
+++ b/solution.py
@@ -10,6 +10,7 @@
 MESH = pl.DeviceIdType.MESH
 SLOTS = 4
 LEAD = 4
+VMEM_BYTES = 38 * 1024 * 1024
 
 
 def sum_order(n):
@@ -100,20 +101,16 @@
             recv_sem=scale_recv.at[group], device_id={"shard": group}, device_id_type=MESH,
         )
 
+    def kept(k):
+        return k - (k > 2)
+
     def data_copy(k, t, e):
         return pltpu.make_async_remote_copy(
-            src_ref=sbuf.at[k, t * per + e],
+            src_ref=sbuf.at[kept(k), t * per + e],
             dst_ref=finals[t].at[e, pl.ds(me * rows, rows)],
             send_sem=data_send.at[k, t * per + e],
             recv_sem=data_recv.at[me, t * per + e],
             device_id={"shard": targets[k]}, device_id_type=MESH,
-        )
-
-    def own_copy(k, t, e):
-        return pltpu.make_async_copy(
-            sbuf.at[k, t * per + e],
-            finals[t].at[e, pl.ds(me * rows, rows)],
-            data_send.at[k, t * per + e],
         )
 
     def data_arrival(source, t, e):
@@ -177,15 +174,16 @@
 
             def block(b, _):
                 start = pl.multiple_of(b * 16, 16)
-                sbuf[k, t * per + e, pl.ds(start, 16), :] = (
-                    ring[slot, e, pl.ds(start, 16), :] * wide
-                ).astype(jnp.bfloat16)
+                value = (ring[slot, e, pl.ds(start, 16), :] * wide).astype(jnp.bfloat16)
+                if k == 2:
+                    base = pl.multiple_of(me * rows + start, 16)
+                    finals[t][e, pl.ds(base, 16), :] = value
+                else:
+                    sbuf[kept(k), t * per + e, pl.ds(start, 16), :] = value
                 return 0
 
             lax.fori_loop(0, rows // 16, block, 0, unroll=4)
-            if k == 2:
-                own_copy(k, t, e).start()
-            else:
+            if k != 2:
                 data_copy(k, t, e).start()
             return 0
 
@@ -206,15 +204,15 @@
         scale_up[...] = scale[per:]
 
     early = me == order[0]
-    for i in range(1, LEAD // 2):
+    for i in range(1, LEAD - 2):
         early = jnp.logical_or(early, me == order[i])
 
     for index, (kind, step, group, t) in enumerate(work):
         slot = index % SLOTS
+        if kind == "sum" and t == 0 and step == LEAD - 1:
+            pl.when(early)(home)
         if kind == "send" and t == 0:
-            if step == 0:
-                pl.when(early)(home)
-            elif step == 1:
+            if step == 1:
                 pl.when(jnp.logical_not(early))(home)
                 routers[mine, me] = (router_t[...] * gain[...]).astype(jnp.bfloat16)
                 for j in range(1, n):
@@ -253,14 +251,11 @@
         row_copy(j).wait_send()
     for j in range(1, ne):
         col_copy(j).wait_send()
-    for k in range(n):
+    for k in [k for k in range(n) if k != 2]:
         for t in (0, 1):
 
             def done(e, _, k=k, t=t):
-                if k == 2:
-                    own_copy(k, t, e).wait()
-                else:
-                    data_copy(k, t, e).wait_send()
+                data_copy(k, t, e).wait_send()
                 return 0
 
             lax.fori_loop(0, per, done, 0)
@@ -272,6 +267,23 @@
                 return 0
 
             lax.fori_loop(0, per, arrived, 0)
+
+
+def place(
+    gate, up, scale_gate, scale_up, router_t,
+    final_gate, final_up, out_gate, out_up, router, sems,
+):
+    copies = [
+        pltpu.make_async_copy(gate, final_gate, sems.at[0]),
+        pltpu.make_async_copy(up, final_up, sems.at[1]),
+    ]
+    for copy in copies:
+        copy.start()
+    out_gate[...] = scale_gate[...]
+    out_up[...] = scale_up[...]
+    router[...] = router_t[...].T
+    for copy in copies:
+        copy.wait()
 
 
 def solution(mesh):
@@ -283,14 +295,16 @@
         router_t = router_weight.T
         wide, tall = router_t.shape
         sem = pltpu.SemaphoreType.DMA
-        final_gate, final_up, scale_gate, scale_up, serve_t = pl.pallas_call(
+        vmem = pl.BlockSpec(memory_space=pltpu.VMEM)
+        hbm = pl.BlockSpec(memory_space=pl.ANY)
+        landed = pl.pallas_call(
             functools.partial(kernel, n, ne, rows * n),
             out_shape=(
-                jax.ShapeDtypeStruct((per, rows * n, cols), jnp.bfloat16),
-                jax.ShapeDtypeStruct((per, rows * n, cols), jnp.bfloat16),
-                jax.ShapeDtypeStruct((per, cols), jnp.float32),
-                jax.ShapeDtypeStruct((per, cols), jnp.float32),
-                jax.ShapeDtypeStruct((wide * ne, tall * n), jnp.bfloat16),
+                pltpu.VMEM((per, rows * n, cols), jnp.bfloat16),
+                pltpu.VMEM((per, rows * n, cols), jnp.bfloat16),
+                pltpu.VMEM((per, cols), jnp.float32),
+                pltpu.VMEM((per, cols), jnp.float32),
+                pltpu.VMEM((wide * ne, tall * n), jnp.bfloat16),
             ),
             in_specs=[
                 pl.BlockSpec(memory_space=pl.ANY),
@@ -298,16 +312,10 @@
                 pl.BlockSpec(memory_space=pltpu.VMEM),
                 pl.BlockSpec(memory_space=pltpu.VMEM),
             ],
-            out_specs=(
-                pl.BlockSpec(memory_space=pl.ANY),
-                pl.BlockSpec(memory_space=pl.ANY),
-                pl.BlockSpec(memory_space=pltpu.VMEM),
-                pl.BlockSpec(memory_space=pltpu.VMEM),
-                pl.BlockSpec(memory_space=pltpu.VMEM),
-            ),
+            out_specs=(vmem,) * 5,
             scratch_shapes=[
                 pltpu.VMEM((SLOTS, per, rows, cols), jnp.float32),
-                pltpu.VMEM((n, 2 * per, rows, cols), jnp.bfloat16),
+                pltpu.VMEM((n - 1, 2 * per, rows, cols), jnp.bfloat16),
                 pltpu.VMEM((n, 2 * per, cols), jnp.float32),
                 pltpu.VMEM((n, 2 * per, cols), jnp.float32),
                 pltpu.VMEM((n, 2 * per, cols), jnp.float32),
@@ -318,10 +326,23 @@
                 sem((n,)), sem((n,)), sem((ne,)), sem((ne,)),
             ],
             compiler_params=pltpu.CompilerParams(
-                collective_id=0, has_side_effects=True, vmem_limit_bytes=60 * 1024 * 1024
+                collective_id=0, has_side_effects=True, vmem_limit_bytes=VMEM_BYTES
             ),
         )(master_gate, master_up, router_t, router_gain[None, :])
-        return final_gate, final_up, scale_gate, scale_up, serve_t.T
+        return pl.pallas_call(
+            place,
+            out_shape=(
+                jax.ShapeDtypeStruct((per, rows * n, cols), jnp.bfloat16),
+                jax.ShapeDtypeStruct((per, rows * n, cols), jnp.bfloat16),
+                jax.ShapeDtypeStruct((per, cols), jnp.float32),
+                jax.ShapeDtypeStruct((per, cols), jnp.float32),
+                jax.ShapeDtypeStruct((tall * n, wide * ne), jnp.bfloat16),
+            ),
+            in_specs=[vmem] * 5,
+            out_specs=(hbm, hbm, vmem, vmem, vmem),
+            scratch_shapes=[sem((2,))],
+            compiler_params=pltpu.CompilerParams(vmem_limit_bytes=8 * 1024 * 1024),
+        )(*landed)
 
     return jax.shard_map(
         body,

time: 593 us -> 580 us (0.978)
  local copies, waits for them, and re-layouts: 21 us -> 0 us
  Pallas kernels: 571 us -> 579 us
    unnamed x11 -> x0, local copies, waits for them, and re-layouts: 21 us -> none
    pallas_call x1 -> x2, Pallas kernels: 571 us -> 579 us  [the longest x1 569 us: body(): pl.pallas_call(functools.partial(kernel, n, ne, rows * n), out_shape=(plt...]
where the time goes in v2:
time: 580 us; the launch traced here: 579 us
  Pallas kernels  579 us (100%)
    pallas_call x1, Pallas kernels, body(): pl.pallas_call(functools.partial(kernel, n, ne, rows * n), out_shape=(plt...  569 us

profile of v2, /device:TPU:1, one launch (start us, length us, event | category | flops | bytes accessed | tf_op | source)
XLA Modules:
  0.0 579.4 jit_solution(770149509670176133)
XLA Ops:
  0.6 569.0 %shard_map.83 = (bf16[4,2048,768]{2,1,0:T(8,128)(2,1)S(1)}, bf16[4,2048,768]{2,1,0:T(8,128)(2,1)S(1)}, f32[4,768]{1,0:T(4,128)S(1)}, f32[4,768]{1,0:T(4,128)S(1)}, bf16[128,2048]{1,0:T(8,128)(2,1)S(1)}) custom-call(f32[32,256,768]{2,1,0:T(8,128)} %gate.1, f32[32,256,768]{2,1,0:T(8,128)} %up.1, f32[32,256]{1,0:T(8,128)} %bitcast.2, f32[1,256]{1,0:T(1,128)} %bitcast.3), custom_call_target="tpu_custom_call" | custom-call | tf_op jit(solution)/shard_map/pallas_call | solution.py:300
  569.7 9.7 %shard_map.84 = (bf16[4,2048,768]{2,1,0:T(8,128)(2,1)}, bf16[4,2048,768]{2,1,0:T(8,128)(2,1)}, f32[4,768]{1,0:T(4,128)}, f32[4,768]{1,0:T(4,128)}, bf16[2048,128]{1,0:T(8,128)(2,1)}) custom-call(bf16[4,2048,768]{2,1,0:T(8,128)(2,1)S(1)} %get-tuple-element.10.gate, bf16[4,2048,768]{2,1,0:T(8,128)(2,1)S(1)} %get-tuple-element.11.up, ...), custom_call_target="tpu_custom_call" | custom-call | tf_op jit(solution)/shard_map/pallas_call | solution.py:332

commit v3 on v2

--- a/solution.py
+++ b/solution.py
@@ -22,7 +22,9 @@
     chip = me // 2
     order = sum_order(n)
     others = [g for g in range(n) if g // 2 != chip]
-    return sorted(others, key=lambda g: (abs(g // 2 - chip), g % 2, order.index(g)))
+    near = sorted(others, key=lambda g: (abs(g // 2 - chip), g % 2, order.index(g)))
+    first = next(g for g in near if g in order[:2])
+    return [first] + [g for g in near if g != first]
 
 
 def pick(me, values):
@@ -36,9 +38,9 @@
     n, ne, rows_total,
     gate, up, router_t, gain,
     final_gate, final_up, scale_gate, scale_up, out_router_t,
-    ring, sbuf, psum, parts, scales, routers,
-    read_sem, psum_send, psum_recv, scale_send, scale_recv,
-    data_send, data_recv, row_send, row_recv, col_send, col_recv,
+    ring, sbuf, psum, parts, pairs, scales, routers,
+    read_sem, psum_send, psum_recv, pair_recv, scale_send, scale_recv, pass_send,
+    data_send, data_recv, row_send, row_recv, half_send, half_recv, col_send, col_recv,
 ):
     me = lax.axis_index("shard")
     mine = lax.axis_index("expert")
@@ -47,9 +49,11 @@
     sources, finals = (gate, up), (final_gate, final_up)
 
     order = sum_order(n)
+    early, late = order[:2], order[2:]
+    core, chip = lax.rem(me, 2), me // 2
     tables = [send_order(n, i) for i in range(n)]
     remote = [pick(me, [tables[i][k] for i in range(n)]) for k in range(n - 2)]
-    partner = me + 1 - 2 * lax.rem(me, 2)
+    partner = me + 1 - 2 * core
     targets = [remote[0], partner, me] + remote[1:]
 
     work = []
@@ -83,16 +87,28 @@
             recv_sem=psum_recv.at[me], device_id={"shard": group}, device_id_type=MESH,
         )
 
+    def pair_copy(group):
+        return pltpu.make_async_remote_copy(
+            src_ref=psum.at[group], dst_ref=pairs.at[group], send_sem=psum_send.at[group],
+            recv_sem=pair_recv.at[group], device_id={"shard": partner}, device_id_type=MESH,
+        )
+
     def psum_arrival(source):
         return pltpu.make_async_remote_copy(
             src_ref=parts.at[source], dst_ref=parts.at[source], send_sem=psum_send.at[source],
             recv_sem=psum_recv.at[source], device_id={"shard": source}, device_id_type=MESH,
         )
 
-    def scale_copy(j):
+    def scale_copy(j, target):
         return pltpu.make_async_remote_copy(
             src_ref=scales.at[me], dst_ref=scales.at[me], send_sem=scale_send.at[j],
-            recv_sem=scale_recv.at[me], device_id={"shard": peer(j)}, device_id_type=MESH,
+            recv_sem=scale_recv.at[me], device_id={"shard": target}, device_id_type=MESH,
+        )
+
+    def scale_pass(group):
+        return pltpu.make_async_remote_copy(
+            src_ref=scales.at[group], dst_ref=scales.at[group], send_sem=pass_send.at[group],
+            recv_sem=scale_recv.at[group], device_id={"shard": partner}, device_id_type=MESH,
         )
 
     def scale_arrival(group):
@@ -124,15 +140,24 @@
 
     def row_copy(j):
         return pltpu.make_async_remote_copy(
-            src_ref=routers.at[mine, me], dst_ref=routers.at[mine, me], send_sem=row_send.at[j],
-            recv_sem=row_recv.at[me], device_id={"shard": peer(j)}, device_id_type=MESH,
-        )
-
-    def row_arrival(source):
-        return pltpu.make_async_remote_copy(
-            src_ref=routers.at[mine, source], dst_ref=routers.at[mine, source],
-            send_sem=row_send.at[0], recv_sem=row_recv.at[source],
+            src_ref=routers.at[mine, core, chip], dst_ref=routers.at[mine, core, chip],
+            send_sem=row_send.at[j], recv_sem=row_recv.at[chip],
+            device_id={"shard": peer(j)}, device_id_type=MESH,
+        )
+
+    def row_arrival(j):
+        source = peer(j)
+        return pltpu.make_async_remote_copy(
+            src_ref=routers.at[mine, core, source // 2], dst_ref=routers.at[mine, core, source // 2],
+            send_sem=row_send.at[j], recv_sem=row_recv.at[source // 2],
             device_id={"shard": source}, device_id_type=MESH,
+        )
+
+    def half_copy(half):
+        return pltpu.make_async_remote_copy(
+            src_ref=routers.at[mine, half], dst_ref=routers.at[mine, half],
+            send_sem=half_send.at[0], recv_sem=half_recv.at[0],
+            device_id={"shard": partner}, device_id_type=MESH,
         )
 
     def col_copy(j):
@@ -189,36 +214,72 @@
 
         lax.fori_loop(0, per, one, 0)
 
-    def home():
-        for j in range(1, n):
-            psum_arrival(peer(j)).wait_recv()
-        parts[me] = psum[me]
-        total = parts[0]
-        for i in range(1, n):
-            total = total + parts[i]
+    def finish(sources):
+        total = psum[me]
+        for source in sources:
+            psum_arrival(source).wait_recv()
+            total = total + parts[source]
         scale = total / rows_total
         scales[me] = scale
-        for j in range(1, n):
-            scale_copy(j).start()
         scale_gate[...] = scale[:per]
         scale_up[...] = scale[per:]
 
-    early = me == order[0]
-    for i in range(1, LEAD - 2):
-        early = jnp.logical_or(early, me == order[i])
+    def home_early():
+        finish([peer(j) for j in range(1, n)])
+        for j in range(1, n):
+            scale_copy(j, peer(j)).start()
+
+    def home_late():
+        finish([peer(j) for j in range(2, n, 2)])
+        scale_copy(1, partner).start()
+        for j in range(2, n, 2):
+            scale_copy(j, peer(j)).start()
+
+    def combine(group):
+        pair_copy(group).wait_recv()
+        psum[group] = psum[group] + pairs[group]
+
+        @pl.when(me != group)
+        def _():
+            psum_copy(group).start()
+
+    is_early = jnp.logical_or(me == early[0], me == early[1])
+
+    def exchange_late():
+        for group in late:
+            pl.when(core == group % 2)(functools.partial(combine, group))
+        pl.when(jnp.logical_not(is_early))(home_late)
+        for group in late:
+
+            @pl.when(jnp.logical_and(core == group % 2, me != group))
+            def _(group=group):
+                scale_arrival(group).wait_recv()
+                scale_pass(group).start()
+
+        for group in late:
+
+            @pl.when(core != group % 2)
+            def _(group=group):
+                scale_arrival(group).wait_recv()
+
+        for group in early:
+
+            @pl.when(jnp.logical_and(me != group, targets[0] != group))
+            def _(group=group):
+                scale_arrival(group).wait_recv()
 
     for index, (kind, step, group, t) in enumerate(work):
         slot = index % SLOTS
         if kind == "sum" and t == 0 and step == LEAD - 1:
-            pl.when(early)(home)
+            pl.when(is_early)(home_early)
         if kind == "send" and t == 0:
-            if step == 1:
-                pl.when(jnp.logical_not(early))(home)
-                routers[mine, me] = (router_t[...] * gain[...]).astype(jnp.bfloat16)
-                for j in range(1, n):
+            if step == 0:
+                scale_arrival(group).wait_recv()
+            elif step == 1:
+                exchange_late()
+                routers[mine, core, chip] = (router_t[...] * gain[...]).astype(jnp.bfloat16)
+                for j in range(2, n, 2):
                     row_copy(j).start()
-            if step != 2:
-                scale_arrival(group).wait_recv()
         read(index).wait()
         if kind == "sum":
             sum_chunk(slot, group, t)
@@ -226,29 +287,53 @@
                 if step == 0:
                     pl.semaphore_wait(barrier, n - 1 + ne - 1)
 
-                @pl.when(me != group)
-                def _(group=group):
-                    psum_copy(group).start()
+                if group in early:
+
+                    @pl.when(me != group)
+                    def _(group=group):
+                        psum_copy(group).start()
+                else:
+
+                    @pl.when(core != group % 2)
+                    def _(group=group):
+                        pair_copy(group).start()
         else:
             send_chunk(slot, step, group, t)
         if index + SLOTS < len(work):
             read(index + SLOTS).start()
 
-    for j in range(1, n):
-        row_arrival(peer(j)).wait_recv()
+    for j in range(2, n, 2):
+        row_arrival(j).wait_recv()
+    half_copy(core).start()
+    half_copy(1 - core).wait_recv()
     for j in range(1, ne):
         col_copy(j).start()
     for j in range(1, ne):
         col_arrival(other(j)).wait_recv()
-    wide, tall = routers.shape[2], routers.shape[3]
+    wide, tall = routers.shape[3], routers.shape[4]
     for e in range(ne):
         for s in range(n):
-            out_router_t[e * wide:(e + 1) * wide, s * tall:(s + 1) * tall] = routers[e, s]
+            out_router_t[e * wide:(e + 1) * wide, s * tall:(s + 1) * tall] = routers[e, s % 2, s // 2]
 
     for j in range(1, n):
         psum_copy(peer(j)).wait_send()
-        scale_copy(j).wait_send()
+    scale_copy(1, partner).wait_send()
+    for j in range(2, n, 2):
+        scale_copy(j, peer(j)).wait_send()
         row_copy(j).wait_send()
+
+    @pl.when(is_early)
+    def _():
+        for j in range(3, n, 2):
+            scale_copy(j, peer(j)).wait_send()
+
+    for group in late:
+
+        @pl.when(jnp.logical_and(core == group % 2, me != group))
+        def _(group=group):
+            scale_pass(group).wait_send()
+
+    half_copy(core).wait_send()
     for j in range(1, ne):
         col_copy(j).wait_send()
     for k in [k for k in range(n) if k != 2]:
@@ -271,18 +356,20 @@
 
 def place(
     gate, up, scale_gate, scale_up, router_t,
-    final_gate, final_up, out_gate, out_up, router, sems,
+    final_gate, final_up, out_gate, out_up, router, turned, sems, small,
 ):
-    copies = [
-        pltpu.make_async_copy(gate, final_gate, sems.at[0]),
-        pltpu.make_async_copy(up, final_up, sems.at[1]),
-    ]
+    copies = []
+    for e in range(gate.shape[0]):
+        copies.append(pltpu.make_async_copy(gate.at[e], final_gate.at[e], sems.at[0, e]))
+        copies.append(pltpu.make_async_copy(up.at[e], final_up.at[e], sems.at[1, e]))
+    copies.append(pltpu.make_async_copy(scale_gate, out_gate, small.at[0]))
+    copies.append(pltpu.make_async_copy(scale_up, out_up, small.at[1]))
     for copy in copies:
         copy.start()
-    out_gate[...] = scale_gate[...]
-    out_up[...] = scale_up[...]
-    router[...] = router_t[...].T
-    for copy in copies:
+    turned[...] = router_t[...].T
+    last = pltpu.make_async_copy(turned, router, small.at[2])
+    last.start()
+    for copy in copies + [last]:
         copy.wait()
 
 
@@ -319,11 +406,12 @@
                 pltpu.VMEM((n, 2 * per, cols), jnp.float32),
                 pltpu.VMEM((n, 2 * per, cols), jnp.float32),
                 pltpu.VMEM((n, 2 * per, cols), jnp.float32),
-                pltpu.VMEM((ne, n, wide, tall), jnp.bfloat16),
+                pltpu.VMEM((n, 2 * per, cols), jnp.float32),
+                pltpu.VMEM((ne, 2, n // 2, wide, tall), jnp.bfloat16),
                 sem((SLOTS,)),
-                sem((n,)), sem((n,)), sem((n,)), sem((n,)),
+                sem((n,)), sem((n,)), sem((n,)), sem((n,)), sem((n,)), sem((n,)),
                 sem((n, 2 * per)), sem((n, 2 * per)),
-                sem((n,)), sem((n,)), sem((ne,)), sem((ne,)),
+                sem((n,)), sem((n // 2,)), sem((1,)), sem((1,)), sem((ne,)), sem((ne,)),
             ],
             compiler_params=pltpu.CompilerParams(
                 collective_id=0, has_side_effects=True, vmem_limit_bytes=VMEM_BYTES
@@ -339,8 +427,10 @@
                 jax.ShapeDtypeStruct((tall * n, wide * ne), jnp.bfloat16),
             ),
             in_specs=[vmem] * 5,
-            out_specs=(hbm, hbm, vmem, vmem, vmem),
-            scratch_shapes=[sem((2,))],
+            out_specs=(hbm,) * 5,
+            scratch_shapes=[
+                pltpu.VMEM((tall * n, wide * ne), jnp.bfloat16), sem((2, per)), sem((3,)),
+            ],
             compiler_params=pltpu.CompilerParams(vmem_limit_bytes=8 * 1024 * 1024),
         )(*landed)
 

time: 580 us -> 581 us (level)
  no operation moved by 1% of the time
where the time goes in v3:
time: 581 us
  Pallas kernels  580 us (100%)
    pallas_call x1, Pallas kernels, body(): pl.pallas_call(functools.partial(kernel, n, ne, rows * n), out_shape=(plt...  571 us

profile of v3, /device:TPU:1, one launch (start us, length us, event | category | flops | bytes accessed | tf_op | source)
XLA Modules:
  0.0 580.5 jit_solution(7721785054465550910)
XLA Ops:
  0.6 571.3 %shard_map.83 = (bf16[4,2048,768]{2,1,0:T(8,128)(2,1)S(1)}, bf16[4,2048,768]{2,1,0:T(8,128)(2,1)S(1)}, f32[4,768]{1,0:T(4,128)S(1)}, f32[4,768]{1,0:T(4,128)S(1)}, bf16[128,2048]{1,0:T(8,128)(2,1)S(1)}) custom-call(f32[32,256,768]{2,1,0:T(8,128)} %gate.1, f32[32,256,768]{2,1,0:T(8,128)} %up.1, f32[32,256]{1,0:T(8,128)} %bitcast.2, f32[1,256]{1,0:T(1,128)} %bitcast.3), custom_call_target="tpu_custom_call" | custom-call | tf_op jit(solution)/shard_map/pallas_call | solution.py:387
  571.9 8.6 %shard_map.84 = (bf16[4,2048,768]{2,1,0:T(8,128)(2,1)}, bf16[4,2048,768]{2,1,0:T(8,128)(2,1)}, f32[4,768]{1,0:T(4,128)}, f32[4,768]{1,0:T(4,128)}, bf16[2048,128]{1,0:T(8,128)(2,1)}) custom-call(bf16[4,2048,768]{2,1,0:T(8,128)(2,1)S(1)} %get-tuple-element.10.gate, bf16[4,2048,768]{2,1,0:T(8,128)(2,1)S(1)} %get-tuple-element.11.up, ...), custom_call_target="tpu_custom_call" | custom-call | tf_op jit(solution)/shard_map/pallas_call | solution.py:420
